TPU v7x, 1024 devices: a whole 4x8x16 slice. The times are simulated.
1024 devices in a mesh: role: 2 (over x_hi), ctx: 32 (over z, core), head: 16 (over x_lo, y).
Axes of the slice: x: 4 (x_hi: 2, x_lo: 2; x = x_hi * 2 + x_lo), y: 8, z: 16, core: 2. Of those that a mesh axis runs over, the one named last changes fastest.
Arguments:
- tokens: bfloat16 [2, 2048, 7168], P('role', 'ctx', 'head'), may hold values from -6 to 6
- latent_cache: bfloat16 [1536, 576], P('ctx'), may hold values from -400 to 400
- offset: int32 [1], replicated, may hold values from 385 to 1536
- bounds: int32 [2048], P('ctx'), may hold values from 1 to 3584
- query_down: bfloat16 [7168, 1536], P('head'), may hold values from -0.0625 to 0.0625
- latent_down_weight: bfloat16 [7168, 576], P('head'), may hold values from -0.0625 to 0.0625
- query_gain: float32 [1536], replicated, may hold values from 0.25 to 1.75
- latent_norm_gain: float32 [512], replicated, may hold values from 0.25 to 1.75
- query_up: bfloat16 [1536, 24576], P(None, 'head'), may hold values from -0.15625 to 0.15625
- key_up_transposed: bfloat16 [128, 128, 512], P('head'), may hold values from -0.5 to 0.5
- value_up_weight: bfloat16 [128, 512, 128], P('head'), may hold values from -0.25 to 0.25
Outputs:
- attended: bfloat16 [2, 2048, 16384], P('role', 'ctx', 'head')
Inputs may be any that keep to these rules, and one draw needn't show every extreme that they name: `bounds`: A continuation row at position p sees keys at positions below p and itself. Cache slots from offset on are unused; the block's tokens sit at positions offset to offset + 2047.
All inputs are finite; a program needn't handle non-finite values.
Results may differ from a plain program's by a relative error of at most 0.02.
Values may be sent and summed in bfloat16 or wider, within the bound.
A program may use at most 64 MiB of HBM per device.

v0:
```python
import jax
import jax.numpy as jnp
from jax import lax
from jax.sharding import PartitionSpec as P

LATENT_WIDTH = 512
ROTARY_DIM = 64
PLAIN_QUERY_DIM = 128
VALUE_HEAD_SIZE = 128


EPS = 1e-06


def cut_along(value, dim, peers):
    dims = value.shape
    blocks = value.reshape(*dims[:dim], peers, dims[dim] // peers, *dims[dim + 1 :])
    return jnp.moveaxis(blocks, dim, 0)


def sent_and_summed(value, axis, dim):
    blocks = cut_along(value, dim, lax.axis_size(axis))
    arrived = lax.all_to_all(blocks, axis, split_axis=0, concat_axis=0, tiled=True)
    return arrived.sum(axis=0)


def in_one_piece(arrays, axis, dim, along):
    both = jnp.concatenate(arrays, axis=along)
    result, at, outs = (sent_and_summed(both, axis, dim), 0, [])
    for a in arrays:
        outs.append(lax.slice_in_dim(result, at, at + a.shape[along], axis=along))
        at += a.shape[along]
    return tuple(outs)


def in_one_piece_2(arrays, axis, dim, along):
    widths = [a.shape[along] for a in arrays]
    both = jnp.concatenate(arrays, axis=along)
    result = lax.all_gather(both, axis, axis=dim, tiled=True)
    return tuple(jnp.split(result, [sum(widths[:k]) for k in range(1, len(widths))], axis=along))


def passed_along(value, axis, steps):
    count = lax.axis_size(axis)
    leading, last = (max(0, -steps), min(count, count - steps))
    return lax.ppermute(value, axis, [(source, source + steps) for source in range(leading, last)])


def root_mean_norm(value_rows, gain):
    return (
        value_rows
        * lax.rsqrt(jnp.mean(value_rows * value_rows, axis=-1, keepdims=True) + EPS)
        * gain
    )


def apply_rotary(value_rows, token_positions):
    half = value_rows.shape[-1] // 2
    freqs = 10000.0 ** (-jnp.arange(half, dtype=jnp.float32) / half)
    angles = token_positions.astype(jnp.float32)[:, None] * freqs[None, :]
    if value_rows.ndim == 3:
        angles = angles[:, None, :]
    first = value_rows[..., :half]
    second_half = value_rows[..., half:]
    cosine = jnp.cos(angles)
    sine = jnp.sin(angles)
    return jnp.concatenate(
        [first * cosine - second_half * sine, first * sine + second_half * cosine], axis=-1
    )


def finish_latents(query_lat, key_value_latent, token_positions, query_gain, latent_norm_gain):
    query_norm = root_mean_norm(query_lat, query_gain).astype(jnp.bfloat16)
    latent_vector = root_mean_norm(key_value_latent[:, :LATENT_WIDTH], latent_norm_gain)
    rotary_key_part = apply_rotary(key_value_latent[:, LATENT_WIDTH:], token_positions)
    return (
        query_norm,
        jnp.concatenate([latent_vector, rotary_key_part], axis=-1).astype(jnp.bfloat16),
    )


def local(
    tokens,
    latent_cache,
    offset,
    bounds,
    query_down,
    latent_down_weight,
    query_gain,
    latent_norm_gain,
    query_up,
    key_up_transposed,
    value_up_weight,
):
    count_of_rows = tokens.shape[1]
    cache_rows = latent_cache.shape[0]
    local_head_count = key_up_transposed.shape[0]
    role_index = lax.axis_index("role")
    block_start = offset[0]
    local_rows = lax.axis_index("ctx") * count_of_rows + jnp.arange(count_of_rows, dtype=jnp.int32)
    token_positions = jnp.where(role_index == 0, block_start + local_rows, bounds)
    inputs = tokens[0]
    query_part = jnp.dot(inputs, query_down, preferred_element_type=jnp.float32)
    kv_part = jnp.dot(inputs, latent_down_weight, preferred_element_type=jnp.float32)
    query_lat, key_value_latent = in_one_piece((query_part, kv_part), "head", 0, 1)
    share_rows = query_lat.shape[0]
    share_pos = lax.dynamic_slice_in_dim(
        token_positions, lax.axis_index("head") * share_rows, share_rows
    )
    query_share, key_share = finish_latents(
        query_lat, key_value_latent, share_pos, query_gain, latent_norm_gain
    )
    query_norm, self_key_row = in_one_piece_2((query_share, key_share), "head", 0, 1)
    queries = jnp.dot(query_norm, query_up, preferred_element_type=jnp.float32)
    queries = queries.reshape(count_of_rows, local_head_count, PLAIN_QUERY_DIM + ROTARY_DIM)
    query_nope = queries[..., :PLAIN_QUERY_DIM].astype(jnp.bfloat16)
    query_rot = apply_rotary(queries[..., PLAIN_QUERY_DIM:], token_positions).astype(jnp.bfloat16)
    absorbed = jnp.einsum(
        "rhn,hnc->rhc", query_nope, key_up_transposed, preferred_element_type=jnp.float32
    ).astype(jnp.bfloat16)
    complete_query = jnp.concatenate([absorbed, query_rot], axis=-1)
    softmax_scale = (PLAIN_QUERY_DIM + ROTARY_DIM) ** (-0.5)
    self_score = jnp.sum(
        complete_query.astype(jnp.float32) * self_key_row.astype(jnp.float32)[:, None, :], axis=-1
    )
    self_score = self_score.reshape(count_of_rows * local_head_count) * softmax_scale
    flattened_query = complete_query.reshape(
        count_of_rows * local_head_count, LATENT_WIDTH + ROTARY_DIM
    )
    row_limits = jnp.repeat(token_positions, local_head_count)
    relayed = passed_along(self_key_row, "role", 1)
    block_key = jnp.where(role_index == 0, self_key_row, relayed)
    per_shard = cache_rows + count_of_rows
    local_keys = jnp.concatenate([latent_cache, block_key], axis=0)
    slice_portion = lax.all_gather(local_keys, "ctx", axis=0, tiled=True)
    global_index = jnp.arange(slice_portion.shape[0], dtype=jnp.int32)
    shard_index = global_index // per_shard
    within = global_index % per_shard
    is_cached = within < cache_rows
    key_pos = jnp.where(
        is_cached,
        shard_index * cache_rows + within,
        block_start + shard_index * count_of_rows + within - cache_rows,
    )
    key_valid = jnp.where(is_cached, key_pos < block_start, True)
    running_max = self_score
    running_sum = jnp.ones_like(self_score)
    output_accumulate = jnp.repeat(
        self_key_row[:, :LATENT_WIDTH].astype(jnp.float32), local_head_count, axis=0
    )
    scores = (
        jnp.dot(flattened_query, slice_portion.T, preferred_element_type=jnp.float32)
        * softmax_scale
    )
    key_mask = key_valid[None, :] & (key_pos[None, :] < row_limits[:, None])
    new_max = jnp.maximum(running_max, jnp.max(jnp.where(key_mask, scores, -jnp.inf), axis=-1))
    attention_weights = jnp.where(key_mask, jnp.exp(scores - new_max[:, None]), 0.0)
    fading = jnp.exp(running_max - new_max)
    running_sum = running_sum * fading + jnp.sum(attention_weights, axis=-1)
    output_accumulate = output_accumulate * fading[:, None] + jnp.dot(
        attention_weights.astype(jnp.bfloat16),
        slice_portion[:, :LATENT_WIDTH],
        preferred_element_type=jnp.float32,
    )
    final_state = (new_max, running_sum, output_accumulate)
    running_max, running_sum, output_accumulate = final_state
    out_latent = (
        (output_accumulate / running_sum[:, None])
        .astype(jnp.bfloat16)
        .reshape(count_of_rows, local_head_count, LATENT_WIDTH)
    )
    result = jnp.einsum(
        "rhc,hcv->rhv", out_latent, value_up_weight, preferred_element_type=jnp.float32
    ).astype(jnp.bfloat16)
    return result.reshape(1, count_of_rows, local_head_count * VALUE_HEAD_SIZE)


def solution(mesh):
    return jax.shard_map(
        local,
        mesh=mesh,
        in_specs=(
            P("role", "ctx", "head"),
            P("ctx", None),
            P(),
            P("ctx"),
            P("head", None),
            P("head", None),
            P(),
            P(),
            P(None, "head"),
            P("head", None, None),
            P("head", None, None),
        ),
        out_specs=P("role", "ctx", "head"),
        check_vma=False,
    )
```

profile of v0, /device:TPU:6, one launch (start us, length us, event | category | flops | bytes accessed | tf_op | source)
XLA Modules:
  0.0 177.8 jit_solution(11702674022068204292)
XLA Ops:
  6.5 0.0 copy-start
  6.5 0.0 copy-start.5
  6.5 0.0 copy-start.4
  6.5 0.0 copy-start.3
  6.5 0.0 copy-start.2
  6.5 1.4 fusion.32
  8.0 0.1 copy-done
  8.1 1.2 fusion.34
  9.3 1.0 reshape.147
  10.3 8.6 %all-to-all-start = ((f32[16,4,2112]{2,1,0:T(4,128)}), f32[16,4,2112]{2,1,0:T(4,128)S(1)}, u32[]{:S(2)}, u32[]{:S(2)}) async-start(f32[16,4,2112]{2,1,0:T(4,128)} %reshape.147), calls=%async_computation | async-start | bytes 1114112 | tf_op jit(solution)/shard_map/all_to_all | solution.py:23
  18.9 0.0 all-gather.3.cloned.1.call-start
  19.6 0.0 copy-done.5
  19.6 0.1 dynamic-slice_convert_fusion
  19.7 14.3 %all-to-all-done = f32[16,4,2112]{2,1,0:T(4,128)S(1)} async-done(((f32[16,4,2112]{2,1,0:T(4,128)}), f32[16,4,2112]{2,1,0:T(4,128)S(1)}, u32[]{:S(2)}, u32[]{:S(2)}) %all-to-all-start) | async-done | bytes 540704 | tf_op jit(solution)/shard_map/all_to_all | solution.py:23
  34.0 0.1 reduce_sum.45
  34.1 0.1 multiply_reduce_fusion.2
  34.2 0.1 multiply_reduce_fusion.1
  34.4 0.1 fusion.49
  34.5 0.0 copy-done.4
  34.5 0.1 multiply_convert_fusion.1
  34.6 0.0 copy-done.3
  34.6 0.1 multiply_convert_fusion
  34.7 0.1 concatenate.19
  34.8 34.6 %all-gather = bf16[16,4,2112]{2,1,0:T(4,128)(2,1)S(1)} all-gather(bf16[1,4,2112]{2,1,0:T(4,128)(2,1)S(1)} %bitcast.35), channel_id=1, replica_groups=mesh['role'=2,'ctx'=32,'head'=16] {'head'}, dimensions={0}, use_global_device_ids=true | all-gather | bytes 287232 | tf_op jit(solution)/shard_map/all_gather | solution.py:39
  69.3 0.1 reshape.154
  69.5 1.3 collective-permute-start
  70.8 7.7 %collective-permute-done = bf16[64,576]{1,0:T(8,128)(2,1)S(1)} collective-permute-done((bf16[64,576]{1,0:T(8,128)(2,1)S(1)}, bf16[64,576]{1,0:T(8,128)(2,1)S(1)}, u32[]{:S(2)}, u32[]{:S(2)}) %collective-permute-start) | collective-permute-done | bytes 73760 | tf_op jit(solution)/shard_map/ppermute | solution.py:46
  78.5 0.0 copy-done.2
  78.5 0.7 pad_maximum_fusion.2
  79.2 0.0 all-gather.3.cloned.1.call-update
  79.3 0.1 broadcast_in_dim.16
  79.3 0.1 lt.55
  79.5 0.2 multiply_cosine_fusion
  79.7 3.3 %fusion.30 = f32[64,1536]{1,0:T(8,128)S(1)} fusion(bf16[1536,1536]{1,0:T(8,128)(2,1)} %param.19, bf16[64,2112]{1,0:T(8,128)(2,1)S(1)} %reshape.154), kind=kOutput, calls=%fused_computation.30 | convolution fusion | flops 301989888 | bytes 5308416 | tf_op jit(solution)/shard_map/dot_general | solution.py:114
  83.0 0.2 reshape.149
  83.2 0.1 fusion.54
  83.3 0.1 subtract_convert_fusion
  83.4 1.5 fusion.15
  84.9 0.3 multiply_reduce_fusion
  85.2 0.1 copy.25
  85.3 0.1 mul.213
  85.4 72.8 %all-gather.3.cloned.1.call-done = bf16[3584,576]{1,0:T(8,128)(2,1)} async-done(((bf16[112,576]{1,0:T(8,128)(2,1)}), bf16[3584,576]{1,0:T(8,128)(2,1)}) %all-gather.3.cloned.1.call-update) | async-done | bytes 4128784 | tf_op jit(solution)/shard_map/all_gather | solution.py:135
  158.2 0.0 slice-start
  158.2 0.0 slice-start.1
  158.2 6.1 %select_reduce_fusion = (f32[512]{0:T(512)S(1)}, f32[512,3584]{1,0:T(8,128)S(1)}) fusion(s32[3584]{0:T(1024)S(1)} %add_select_fusion.2, s32[512]{0:T(512)S(1)} %lt.55, pred[3584]{0:T(1024)(128)(4,1)S(1)} %compare_select_fusion, bf16[3584,576]{1,0:T(8,128)(2,1)} %all-gather.3.cloned.1.call-done, bf16[64,8,576]{2,0,1:T(8,128)(2,1)S(1)} %get-tuple-element.8), kind=kOutput, calls=%fused_computation.1 | convolution fusion | flops 2123103744 | bytes 12080640 | tf_op jit(solution)/shard_map/dot_general | solution.py:152
  164.4 2.9 %fusion = f32[512]{0:T(512)S(1)} fusion(f32[512,3584]{1,0:T(8,128)S(1)} %get-tuple-element.22, f32[512]{0:T(512)S(1)} %max.13, s32[3584]{0:T(1024)S(1)} %add_select_fusion.2, s32[512]{0:T(512)S(1)} %lt.55, pred[3584]{0:T(1024)(128)(4,1)S(1)} %compare_select_fusion), kind=kLoop, calls=%fused_computation.3 | loop fusion | flops 11009536 | bytes 7364096 | tf_op jit(solution)/shard_map/reduce_sum | solution.py:159
  167.3 0.0 slice-done
  167.3 0.0 slice-done.1
  167.3 0.0 copy-start.1
  167.3 2.4 %fusion.21 = bf16[64,8,512]{2,1,0:T(8,128)(2,1)S(1)} fusion(bf16[3584,576]{1,0:T(8,128)(2,1)S(1)} %bitcast.37, f32[512,3584]{1,0:T(8,128)S(1)} %get-tuple-element.22, f32[512]{0:T(512)S(1)} %max.13, s32[3584]{0:T(1024)S(1)} %add_select_fusion.2, s32[512]{0:T(512)S(1)} %lt.55, pred[3584]{0:T(1024)(128)(4,1)S(1)} %compare_select_fusion, ...), kind=kOutput, calls=%fused_computation.20 | convolution fusion | flops 1891106816 | bytes 11694080 | tf_op jit(solution)/shard_map/dot_general | solution.py:160
  169.7 0.0 copy-done.1
  169.7 0.4 fusion.16
  170.1 0.1 copy.28
  170.2 0.7 reshape.152
  (15 shorter events, 0.2 us)
Async XLA Ops:
  6.5 1.5 copy-start
  6.5 13.0 %copy-start.5 = (s32[64]{0:T(128)S(1)}, s32[64]{0:T(128)}, u32[]{:S(2)}) copy-start(s32[64]{0:T(128)} %param.14) | copy-start | bytes 772
  6.5 28.0 %copy-start.4 = (f32[512]{0:T(512)S(1)}, f32[512]{0:T(512)}, u32[]{:S(2)}) copy-start(f32[512]{0:T(512)} %param.18) | copy-start | bytes 6148
  6.5 28.0 %copy-start.3 = (f32[1536]{0:T(1024)S(1)}, f32[1536]{0:T(1024)}, u32[]{:S(2)}) copy-start(f32[1536]{0:T(1024)} %param.17) | copy-start | bytes 18436
  6.5 72.0 %copy-start.2 = (bf16[48,576]{1,0:T(8,128)(2,1)S(1)}, bf16[48,576]{1,0:T(8,128)(2,1)}, u32[]{:S(2)}) copy-start(bf16[48,576]{1,0:T(8,128)(2,1)} %param.12) | copy-start | bytes 165892
  10.3 23.7 %all-to-all-start = ((f32[16,4,2112]{2,1,0:T(4,128)}), f32[16,4,2112]{2,1,0:T(4,128)S(1)}, u32[]{:S(2)}, u32[]{:S(2)}) async-start(f32[16,4,2112]{2,1,0:T(4,128)} %reshape.147), calls=%async_computation | async-start | bytes 1114112 | tf_op jit(solution)/shard_map/all_to_all | solution.py:23
  18.9 139.4 %all-gather.3.cloned.1.call-start = ((), (), s32[]{:S(2)}) async-start(), calls=%async_computation.1 | async-start | bytes 4730880 | tf_op jit(solution)/shard_map/all_gather | solution.py:135
  69.5 9.0 %collective-permute-start = (bf16[64,576]{1,0:T(8,128)(2,1)S(1)}, bf16[64,576]{1,0:T(8,128)(2,1)S(1)}, u32[]{:S(2)}, u32[]{:S(2)}) collective-permute-start(bf16[64,576]{1,0:T(8,128)(2,1)S(1)} %split.9), channel_id=1, source_target_pairs={{0,512},{1,513},{2,514},{3,515},{4,516},{5,517},{6,518},{7,519},{8... | collective-permute-start | bytes 221192 | tf_op jit(solution)/shard_map/ppermute | solution.py:46
  158.2 9.1 %slice-start = ((s8[4587520]{0:T(1024)(128)(4,1)}), s8[4194304]{0:T(1024)(128)(4,1)S(1)}, s32[]{:S(2)}) async-start(s8[4587520]{0:T(1024)(128)(4,1)} %bitcast.36), calls=%async_computation.2 | async-start | bytes 8388608
  158.2 9.1 %slice-start.1 = ((s8[4587520]{0:T(1024)(128)(4,1)}), s8[393216]{0:T(1024)(128)(4,1)S(1)}, s32[]{:S(2)}) async-start(s8[4587520]{0:T(1024)(128)(4,1)} %bitcast.36), calls=%async_computation.3 | async-start | bytes 786432
  167.3 2.4 %copy-start.1 = (bf16[8,512,128]{2,1,0:T(8,128)(2,1)S(1)}, bf16[8,512,128]{2,1,0:T(8,128)(2,1)}, u32[]{:S(2)}) copy-start(bf16[8,512,128]{2,1,0:T(8,128)(2,1)} %param.21) | copy-start | bytes 3145732
Sparse Core Ops, SparseCore 0:
  79.4 78.8 all-gather.2
where the time goes:
time: 179 us; the launch traced here: 178 us
  waiting for transfers between devices  94.9 us (53%)
  blocking collectives  34.6 us (19%)
  matrix products  16.3 us (9%)
  between operations  14.3 us (8%)
  starting transfers between devices  9.91 us (6%)
  other arithmetic  5.01 us (3%)
  local copies, waits for them, and re-layouts  2.78 us (2%)
    all_gather x1, waiting for transfers between devices, local(): slice_portion = lax.all_gather(local_keys, 'ctx', axis=0, tiled=True)  72.8 us
    all_gather x1, blocking collectives, in_one_piece_2(): result = lax.all_gather(both, axis, axis=dim, tiled=True)  34.6 us
    all_to_all x1, waiting for transfers between devices, sent_and_summed(): lax.all_to_all(blocks, axis, split_axis=0, concat_axis=0, tiled=True)  14.3 us
    all_to_all x1, starting transfers between devices, sent_and_summed(): lax.all_to_all(blocks, axis, split_axis=0, concat_axis=0, tiled=True)  8.58 us
    ppermute x1, waiting for transfers between devices, passed_along(): lax.ppermute(value, axis, [(source, source + steps) for source in range(l...  7.75 us
    dot_general x1, matrix products, local(): jnp.dot(flattened_query, slice_portion.T, preferred_element_type=jnp.floa...  6.15 us
  transfers between devices with their start and end apart: 3, of which 3 were waited for; matrix products, arithmetic and copies ran while one was open for 3% of the time, Pallas kernels for 0%

commit v1 on v0

v1 whole, which is shorter than its diff:
```python
import jax
import jax.numpy as jnp
import numpy as np
from jax import lax
from jax.experimental import pallas as pl
from jax.experimental.pallas import tpu as pltpu
from jax.sharding import PartitionSpec as P

LAT = 512
ROT = 64
KEY = LAT + ROT
NOPE = 128
VAL = 128
HEADS = 8
ROWS = 64
CROWS = 48
QRANK = 1536
QBLOCKS = QRANK // 128
ZS = 16
NCTX = 2 * ZS
NHEAD = 16
EPS = 1e-06
SCALE = (NOPE + ROT) ** (-0.5)
NEG = -1e30
MESH = pl.DeviceIdType.MESH
F32 = jnp.float32
BF16 = jnp.bfloat16
SUBS = 2
PIECE = ROWS // SUBS
QCOLS = HEADS * ROWS
scope = jax.named_scope


def remote(src, dst, send, recv, **where):
    return pltpu.make_async_remote_copy(
        src_ref=src, dst_ref=dst, send_sem=send, recv_sem=recv, device_id=where, device_id_type=MESH
    )


def swap_halves(v):
    return jnp.concatenate([v[:, ROT // 2 :], v[:, : ROT // 2]], axis=1)


def body(
    tokens, cache, query_down, latent_down, query_up, key_up,
    offset, bounds, freqs, query_gain, latent_gain,
    out,
    xv, ldv, qdv, qupv, kupv, cos, sin,
    stage_kv, stage_q, rs_kv, rs_q, qc, ks, kc, kb, qn, qs, m_ref, l_ref, acc,
    load_sem, rs_send, rs_recv, qag_send, qag_recv, kag_send, kag_recv,
    cz_send, cz_recv, cp_send, cp_recv, bz_send, bz_recv, bp_send, bp_recv,
    ready_z, ready_role,
):
    role = lax.axis_index("role")
    c = lax.axis_index("ctx")
    h = lax.axis_index("head")
    z, core = c // 2, c % 2
    up, down = (c + 2) % NCTX, (c + NCTX - 2) % NCTX
    partner = c + 1 - 2 * core
    group = h // 4
    is_kv = h % 4 == 3
    q_block = 3 * group + h % 4
    tail = []

    loads = [
        pltpu.make_async_copy(src, dst, load_sem.at[i])
        for i, (src, dst) in enumerate(
            [
                (tokens.at[0], xv),
                (latent_down, ldv),
                (query_down, qdv),
                (cache, kc.at[pl.ds(0, CROWS)]),
                (query_up, qupv),
                (key_up, kupv),
            ]
        )
    ]
    for copy in loads:
        copy.start()

    barrier = pltpu.get_barrier_semaphore()

    def greet(**where):
        pl.semaphore_signal(barrier, inc=1, device_id=where, device_id_type=MESH)

    for d in range(1, NHEAD):
        greet(head=(h + d) % NHEAD)
    greet(ctx=partner)

    @pl.when(z < ZS - 1)
    def _():
        greet(ctx=up)

    @pl.when(z == 0)
    def _():
        greet(ctx=down)

    gives = (1 - role) * ((h % 4) // 3)

    @pl.when(gives == 1)
    def _():
        for p in range(NHEAD):
            greet(role=1, head=p)

    first = offset[0]
    lane = lax.broadcasted_iota(jnp.int32, (1, ROWS), 1)
    place_row = jnp.where(role == 0, first + c * ROWS + lane, bounds[...].reshape(1, ROWS))
    limits = jnp.concatenate([place_row] * HEADS, axis=1)
    square = (ROWS, ROWS)
    eye = lax.broadcasted_iota(jnp.int32, square, 0) == lax.broadcasted_iota(jnp.int32, square, 1)
    place_col = jnp.sum(jnp.where(eye, place_row.astype(F32), 0.0), axis=1, keepdims=True)
    angles = place_col * freqs[...]
    cos[...] = jnp.cos(angles)
    sines = jnp.sin(angles)
    sin[...] = jnp.where(lax.broadcasted_iota(jnp.int32, square, 1) < ROT // 2, -sines, sines)

    with scope("w_x"):
        loads[0].wait()
        loads[1].wait()
    x = xv[...]
    stage_kv[...] = jnp.dot(x, ldv[...], preferred_element_type=F32).astype(BF16)
    loads[2].wait()
    for i in range(QBLOCKS // 2):
        part = jnp.dot(x, qdv[:, 256 * i : 256 * i + 256], preferred_element_type=F32)
        stage_q[2 * i] = part[:, :128]
        stage_q[2 * i + 1] = part[:, 128:]
    loads[3].wait()
    with scope("w_bar"):
        pl.semaphore_wait(barrier, NHEAD + jnp.minimum(z, 1) + z // (ZS - 1) + 4 * role)

    @pl.when(z > 0)
    def _():
        pl.semaphore_signal(ready_z.at[0], inc=1, device_id={"ctx": down}, device_id_type=MESH)

    @pl.when(z == ZS - 1)
    def _():
        pl.semaphore_signal(ready_z.at[1], inc=1, device_id={"ctx": up}, device_id_type=MESH)

    @pl.when(role == 1)
    def _():
        for g in range(4):
            pl.semaphore_signal(
                ready_role.at[0], inc=1, device_id={"role": 0, "head": 4 * g + 3}, device_id_type=MESH
            )

    def cache_rows(s, sub):
        if s == 8:
            s, sub = 0, sub + 1
        return kc.at[pl.ds(s * 4 * CROWS + sub * CROWS, CROWS)]

    def cache_z(s, d):
        return remote(
            cache_rows(s, 0 if s == 0 else d), cache_rows(s + 1, d),
            cz_send.at[8 * d + s], cz_recv.at[8 * d + s], ctx=(up, down)[d],
        )

    def cache_p(s, d):
        return remote(
            cache_rows(s, d), cache_rows(s, 2 + d),
            cp_send.at[9 * d + s], cp_recv.at[9 * d + s], ctx=partner,
        )

    last = (8, 7)

    def start(copy):
        copy.start()
        tail.append(copy)

    def cache_step(s):
        for d in range(2):
            if 0 < s <= last[d]:
                cache_z(s - 1, d).wait_recv()
            if s < last[d]:
                start(cache_z(s, d))
            if s <= last[d] and (s > 0 or d == 0):
                start(cache_p(s, d))

    for d in range(4):
        g = (group + d) % 4
        owner = 4 * g + 3
        copy = remote(
            stage_kv.at[pl.ds(pl.multiple_of(16 * g, 16), 16)], rs_kv.at[h],
            rs_send.at[d], rs_recv.at[h], head=owner,
        )

        @pl.when(owner != h)
        def _():
            copy.start()

        tail.append((owner != h, copy))

    for d in range(QBLOCKS):
        b = (3 * group + jnp.minimum(h % 4, 2) + d) % QBLOCKS
        owner = 4 * (b // 3) + b % 3
        copy = remote(stage_q.at[b], rs_q.at[h], rs_send.at[4 + d], rs_recv.at[h], head=owner)

        @pl.when(owner != h)
        def _():
            copy.start()

        tail.append((owner != h, copy))

    with scope("c0"):

        @pl.when(z < ZS - 1)
        def _():
            pl.semaphore_wait(ready_z.at[0], 1)

        start(cache_z(0, 0))
        start(cache_p(0, 0))

        @pl.when(z > 0)
        def _():
            cache_z(0, 1).start()

    @pl.when(is_kv)
    def _():
        rows = pl.ds(pl.multiple_of(16 * group, 16), 16)
        total = stage_kv[rows, :].astype(F32)
        for d in range(1, NHEAD):
            p = (h + d) % NHEAD
            with scope("w_rskv"):
                remote(rs_kv.at[p], rs_kv.at[p], rs_send.at[0], rs_recv.at[p], head=p).wait_recv()
                total += rs_kv[p].astype(F32)
        lat, rot = total[:, :LAT], total[:, LAT:]
        lat = lat * lax.rsqrt(jnp.mean(lat * lat, axis=-1, keepdims=True) + EPS) * latent_gain[...].reshape(1, LAT)
        rot = rot * cos[rows, :] + swap_halves(rot) * sin[rows, :]
        ks[0, rows, :LAT] = lat.astype(BF16)
        ks[0, rows, LAT:] = rot.astype(BF16)
        mine = ks.at[0, rows]

        for d in range(1, NHEAD):
            remote(
                mine, ks.at[0, rows], kag_send.at[d], kag_recv.at[group], head=(h + d) % NHEAD
            ).start()

    @pl.when(jnp.logical_not(is_kv))
    def _():
        total = stage_q[q_block]
        for d in range(1, NHEAD):
            p = (h + d) % NHEAD
            with scope("w_rsq"):
                remote(rs_q.at[p], rs_q.at[p], rs_send.at[0], rs_recv.at[p], head=p).wait_recv()
                total += rs_q[p]
        qc[q_block] = total
        for d in range(1, NHEAD):
            remote(
                qc.at[q_block], qc.at[q_block], qag_send.at[d], qag_recv.at[q_block],
                head=(h + d) % NHEAD,
            ).start()

    with scope("c12"):

        @pl.when(z == 0)
        def _():
            pl.semaphore_wait(ready_z.at[1], 1)
            cache_z(0, 1).start()

        tail.append(cache_z(0, 1))
        cache_step(1)
        cache_step(2)

    with scope("role"):

        @pl.when(gives == 1)
        def _():
            rows = pl.ds(pl.multiple_of(16 * group, 16), 16)
            pl.semaphore_wait(ready_role.at[0], NHEAD)
            for d in range(NHEAD):
                remote(
                    ks.at[0, rows], ks.at[1, rows], kag_send.at[NHEAD + d], kag_recv.at[4 + group],
                    role=1, head=(h + d) % NHEAD,
                ).start()

    for g in range(4):
        piece = ks.at[0, pl.ds(16 * g, 16)]

        with scope("w_agkv"):

            @pl.when(h != 4 * g + 3)
            def _():
                remote(piece, piece, kag_send.at[0], kag_recv.at[g], head=4 * g + 3).wait_recv()

    @pl.when(role == 1)
    def _():
        for g in range(4):
            piece = ks.at[1, pl.ds(16 * g, 16)]
            with scope("w_agkv1"):
                remote(piece, piece, kag_send.at[0], kag_recv.at[4 + g], role=0, head=4 * g + 3).wait_recv()

    def block_rows(s, sub, k):
        if s == 8:
            s, sub = 0, sub + 1
        return kb.at[s, pl.ds(sub * ROWS + k * PIECE, PIECE)]

    def block_z(s, d, k):
        i = (8 * d + s) * SUBS + k
        src = ks.at[role, pl.ds(k * PIECE, PIECE)] if s == 0 else block_rows(s, d, k)
        return remote(src, block_rows(s + 1, d, k), bz_send.at[i], bz_recv.at[i], ctx=(up, down)[d])

    def block_p(s, d, k):
        i = (9 * d + s) * SUBS + k
        src = ks.at[role, pl.ds(k * PIECE, PIECE)] if s == 0 else block_rows(s, d, k)
        return remote(src, block_rows(s, 2 + d, k), bp_send.at[i], bp_recv.at[i], ctx=partner)

    def block_step(s):
        for k in range(SUBS):
            for d in range(2):
                if 0 < s <= last[d]:
                    block_z(s - 1, d, k).wait_recv()
                if s < last[d]:
                    start(block_z(s, d, k))
                if s <= last[d] and (s > 0 or d == 0):
                    start(block_p(s, d, k))

    block_step(0)
    kb[0, :ROWS] = ks[role]
    for s in range(1, 6):
        with scope(f"bc{s}"):
            block_step(s)
            cache_step(s + 2)

    for b in range(QBLOCKS):
        with scope("w_agq"):

            @pl.when(h != 4 * (b // 3) + b % 3)
            def _():
                remote(qc.at[b], qc.at[b], qag_send.at[0], qag_recv.at[b], head=4 * (b // 3) + b % 3).wait_recv()

    squares = jnp.zeros((ROWS, 128), F32)
    for b in range(QBLOCKS):
        v = qc[b]
        squares += v * v
    inverse = lax.rsqrt(jnp.sum(squares, axis=-1, keepdims=True) * (1.0 / QRANK) + EPS)
    for b in range(QBLOCKS):
        gain = query_gain[pl.ds(128 * b, 128)].reshape(1, 128)
        qn[:, 128 * b : 128 * b + 128] = (qc[b] * inverse * gain).astype(BF16)

    loads[4].wait()
    loads[5].wait()

    def two_heads(i):
        wide = NOPE + ROT
        q = jnp.dot(qn[...], qupv[:, 2 * wide * i : 2 * wide * (i + 1)], preferred_element_type=F32)
        for j in range(2):
            n = 2 * i + j
            rows = slice(ROWS * n, ROWS * (n + 1))
            nope = q[:, wide * j : wide * j + NOPE].astype(BF16)
            rot = q[:, wide * j + NOPE : wide * (j + 1)]
            qs[rows, LAT:] = (rot * cos[...] + swap_halves(rot) * sin[...]).astype(BF16)
            qs[rows, :LAT] = jnp.dot(nope, kupv[n], preferred_element_type=F32).astype(BF16)

    def score_of(keys):
        return SCALE * lax.dot_general(
            keys, qs[...], (((1,), (1,)), ((), ())), preferred_element_type=F32
        )

    def weighted(keys, e):
        return lax.dot_general(
            keys[:, :LAT], e.astype(BF16), (((0,), (0,)), ((), ())), preferred_element_type=F32
        )

    def attend_self():
        keys = ks[0]
        wide = (ROWS, QCOLS)
        own = lax.broadcasted_iota(jnp.int32, wide, 0) == lax.broadcasted_iota(jnp.int32, wide, 1) % ROWS
        m_ref[...] = jnp.sum(jnp.where(own, score_of(keys), 0.0), axis=0, keepdims=True)
        l_ref[...] = jnp.where(lax.broadcasted_iota(jnp.int32, l_ref.shape, 0) == 0, 1.0, 0.0)
        acc[...] = weighted(keys, jnp.where(own, 1.0, 0.0))

    def attend(keys, bases, rows, edge):
        score = score_of(keys)
        row = lax.broadcasted_iota(jnp.int32, (rows, QCOLS), 0)
        score = jnp.concatenate(
            [
                jnp.where(row < edge - base, score[rows * i : rows * (i + 1)], NEG)
                for i, base in enumerate(bases)
            ],
            axis=0,
        )
        old = m_ref[...]
        new = jnp.maximum(old, jnp.max(score, axis=0, keepdims=True))
        fade = jnp.exp(old - new)
        e = jnp.exp(score - new)
        l_ref[...] = l_ref[...] * fade + jnp.sum(e.reshape(-1, 8, QCOLS), axis=0)
        m_ref[...] = new
        acc[...] = acc[...] * fade + weighted(keys, e)

    def place(s, sub):
        if sub % 2 == 0:
            at = z + ZS - s
        else:
            at = z + s + jnp.where(s == 0, ZS // 2, 0)
        return 2 * (at % ZS) + (core if sub < 2 else 1 - core)

    def cache_attend(j):
        bases = [place(2 * j + i // 4, i % 4) * CROWS for i in range(8)]
        keys = kc[pl.ds(pl.multiple_of(j * 8 * CROWS, 16), 8 * CROWS), :]
        attend(keys, bases, CROWS, jnp.minimum(limits, first))

    def block_attend(s):
        attend(kb[s], [first + place(s, i) * ROWS for i in range(4)], ROWS, limits)

    def cache_partner_wait(s):
        for d in range(2):
            if s <= last[d] and (s > 0 or d == 0):
                cache_p(s, d).wait_recv()

    def block_partner_wait(s):
        for d in range(2):
            if s <= last[d] and (s > 0 or d == 0):
                for k in range(SUBS):
                    block_p(s, d, k).wait_recv()

    with scope("h"):
        for i in range(4):
            two_heads(i)
    with scope("b6"):
        block_step(6)
        cache_step(8)
    with scope("self"):
        attend_self()
    with scope("cpw"):
        for s in range(9):
            cache_partner_wait(s)
    with scope("ca01"):

        @pl.loop(0, 2)
        def _(j):
            cache_attend(j)

    with scope("b7"):
        block_step(7)
    with scope("ca23"):

        @pl.loop(2, 4)
        def _(j):
            cache_attend(j)

    with scope("b8"):
        block_step(8)
        for s in range(1, 7):
            block_partner_wait(s)
    with scope("ba16"):

        @pl.loop(1, 7)
        def _(s):
            block_attend(s)

    with scope("bpw"):
        for s in (7, 0, 8):
            block_partner_wait(s)
    with scope("ba78"):

        @pl.loop(7, 9)
        def _(s):
            block_attend(s % 8)

    out[...] = (acc[...] / jnp.sum(l_ref[...], axis=0, keepdims=True)).astype(BF16)

    for item in tail:
        if isinstance(item, tuple):

            @pl.when(item[0])
            def _():
                item[1].wait_send()

        else:
            item.wait_send()

    @pl.when(is_kv)
    def _():
        mine = ks.at[0, pl.ds(pl.multiple_of(16 * group, 16), 16)]
        for d in range(1, NHEAD):
            remote(mine, mine, kag_send.at[d], kag_recv.at[0], head=(h + d) % NHEAD).wait_send()

        @pl.when(role == 0)
        def _():
            for d in range(NHEAD):
                remote(
                    mine, mine, kag_send.at[NHEAD + d], kag_recv.at[0], role=1, head=(h + d) % NHEAD
                ).wait_send()

    @pl.when(jnp.logical_not(is_kv))
    def _():
        for d in range(1, NHEAD):
            remote(
                qc.at[q_block], qc.at[q_block], qag_send.at[d], qag_recv.at[0], head=(h + d) % NHEAD
            ).wait_send()


def values(olat, value_up, out):
    for n in range(HEADS):
        out[:, VAL * n : VAL * (n + 1)] = lax.dot_general(
            olat[:, ROWS * n : ROWS * (n + 1)], value_up[n], (((0,), (0,)), ((), ())),
            preferred_element_type=F32,
        ).astype(BF16)


def local(
    tokens, latent_cache, offset, bounds, query_down, latent_down_weight, query_gain,
    latent_norm_gain, query_up, key_up_transposed, value_up_weight,
):
    freqs = (10000.0 ** (-np.arange(ROT // 2) / (ROT // 2))).astype(np.float32)
    freqs = jnp.asarray(np.concatenate([freqs, freqs])[None, :])

    anywhere = pl.BlockSpec(memory_space=pl.ANY)
    vmem = pl.BlockSpec(memory_space=pltpu.VMEM)
    smem = pl.BlockSpec(memory_space=pltpu.SMEM)
    dma = lambda n: pltpu.SemaphoreType.DMA((n,))
    wide = HEADS * (NOPE + ROT)
    olat = pl.pallas_call(
        body,
        out_shape=jax.ShapeDtypeStruct((LAT, QCOLS), BF16),
        in_specs=[anywhere] * 6 + [smem] + [vmem] * 4,
        out_specs=vmem,
        scratch_shapes=[
            pltpu.VMEM((ROWS, tokens.shape[2]), BF16),
            pltpu.VMEM((tokens.shape[2], KEY), BF16),
            pltpu.VMEM((tokens.shape[2], QRANK), BF16),
            pltpu.VMEM((QRANK, wide), BF16),
            pltpu.VMEM((HEADS, NOPE, LAT), BF16),
            pltpu.VMEM((ROWS, ROT), F32),
            pltpu.VMEM((ROWS, ROT), F32),
            pltpu.VMEM((ROWS, KEY), BF16),
            pltpu.VMEM((QBLOCKS, ROWS, 128), F32),
            pltpu.VMEM((NHEAD, 16, KEY), BF16),
            pltpu.VMEM((NHEAD, ROWS, 128), F32),
            pltpu.VMEM((QBLOCKS, ROWS, 128), F32),
            pltpu.VMEM((2, ROWS, KEY), BF16),
            pltpu.VMEM((NCTX * CROWS, KEY), BF16),
            pltpu.VMEM((8, 4 * ROWS, KEY), BF16),
            pltpu.VMEM((ROWS, QRANK), BF16),
            pltpu.VMEM((QCOLS, KEY), BF16),
            pltpu.VMEM((1, QCOLS), F32),
            pltpu.VMEM((8, QCOLS), F32),
            pltpu.VMEM((LAT, QCOLS), F32),
            dma(6), dma(16), dma(16), dma(16), dma(12), dma(32), dma(8),
            dma(16), dma(16), dma(18), dma(18),
            dma(16 * SUBS), dma(16 * SUBS), dma(18 * SUBS), dma(18 * SUBS),
            pltpu.SemaphoreType.REGULAR((2,)), pltpu.SemaphoreType.REGULAR((1,)),
        ],
        compiler_params=pltpu.CompilerParams(
            collective_id=0, has_side_effects=True, vmem_limit_bytes=56 * 1024 * 1024
        ),
    )(
        tokens, latent_cache, query_down, latent_down_weight, query_up, key_up_transposed,
        offset, bounds, freqs, query_gain, latent_norm_gain,
    )
    result = pl.pallas_call(
        values,
        out_shape=jax.ShapeDtypeStruct((ROWS, HEADS * VAL), BF16),
        in_specs=[vmem, vmem],
        out_specs=vmem,
    )(olat, value_up_weight)
    return result[None]


def solution(mesh):
    return jax.shard_map(
        local,
        mesh=mesh,
        in_specs=(
            P("role", "ctx", "head"),
            P("ctx", None),
            P(),
            P("ctx"),
            P("head", None),
            P("head", None),
            P(),
            P(),
            P(None, "head"),
            P("head", None, None),
            P("head", None, None),
        ),
        out_specs=P("role", "ctx", "head"),
        check_vma=False,
    )
```

time: 179 us -> 89.4 us (0.50)
  waiting for transfers between devices: 94.9 us -> 0 us
  Pallas kernels: 0 us -> 87.7 us
  blocking collectives: 34.6 us -> 0 us
  matrix products: 16.3 us -> 0 us
  between operations: 14.3 us -> 0.66 us
  starting transfers between devices: 9.91 us -> 0 us
  other arithmetic: 5.01 us -> 0 us
  local copies, waits for them, and re-layouts: 2.78 us -> 0 us
    pallas_call x0 -> x2, Pallas kernels: none -> 87.7 us  [the longest x1 85 us: local(): pl.pallas_call(body, out_shape=jax.ShapeDtypeStruct((LAT, QCOLS), BF16),...]
    all_gather x1 -> x0, waiting for transfers between devices: 72.8 us -> none  [local(): slice_portion = lax.all_gather(local_keys, 'ctx', axis=0, tiled=True)]
    all_gather x1 -> x0, blocking collectives: 34.6 us -> none  [in_one_piece_2(): result = lax.all_gather(both, axis, axis=dim, tiled=True)]
    dot_general x7 -> x0, matrix products: 16.3 us -> none  [the longest x1 6.15 us: local(): jnp.dot(flattened_query, slice_portion.T, preferred_element_type=jnp.floa...]
    all_to_all x1 -> x0, waiting for transfers between devices: 14.3 us -> none  [sent_and_summed(): lax.all_to_all(blocks, axis, split_axis=0, concat_axis=0, tiled=True)]
    all_to_all x1 -> x0, starting transfers between devices: 8.58 us -> none  [sent_and_summed(): lax.all_to_all(blocks, axis, split_axis=0, concat_axis=0, tiled=True)]
    ppermute x1 -> x0, waiting for transfers between devices: 7.75 us -> none  [passed_along(): lax.ppermute(value, axis, [(source, source + steps) for source in range(l...]
    reduce_sum x5 -> x0, other arithmetic: 3.52 us -> none  [the longest x1 2.89 us: local(): running_sum = running_sum * fading + jnp.sum(attention_weights, axis=-1)]
  transfers between devices with their start and end apart: 3 -> 0, of which waited for: 3 -> 0; matrix products, arithmetic and copies ran while one was open for 3% -> 0% of each run, Pallas kernels for 0% -> 0%
where the time goes in v1:
time: 89.4 us; the launch traced here: 88.4 us
  Pallas kernels  87.7 us (98%)
    pallas_call x1, Pallas kernels, local(): pl.pallas_call(body, out_shape=jax.ShapeDtypeStruct((LAT, QCOLS), BF16),...  85 us
    pallas_call x1, Pallas kernels, local(): pl.pallas_call(values, out_shape=jax.ShapeDtypeStruct((ROWS, HEADS * VAL)...  2.75 us

profile of v1, /device:TPU:6, one launch (start us, length us, event | category | flops | bytes accessed | tf_op | source)
XLA Modules:
  0.0 88.4 jit_solution(17517132420359092045)
XLA Ops:
  0.7 85.0 %shard_map.118.olat = bf16[512,512]{1,0:T(8,128)(2,1)} custom-call(bf16[1,64,448]{2,1,0:T(8,128)(2,1)} %tokens.1, bf16[48,576]{1,0:T(8,128)(2,1)} %cache.1, bf16[448,1536]{1,0:T(8,128)(2,1)} %query_down.1, bf16[448,576]{1,0:T(8,128)(2,1)} %latent_down.1, bf16[1536,1536]{1,0:T(8,128)(2,1)} %query_up.1, bf16[8,128,512]{2,1,0:T(8,128)(2,1)} %key_up.1, ...), custom_call_target="tpu_custom_call" | custom-call | tf_op jit(solution)/shard_map/pallas_call | solution.py:512
  85.6 2.8 %shard_map.119 = bf16[64,1024]{1,0:T(8,128)(2,1)} custom-call(bf16[512,512]{1,0:T(8,128)(2,1)} %shard_map.118.olat, bf16[8,512,128]{2,1,0:T(8,128)(2,1)} %value_up.1), custom_call_target="tpu_custom_call" | custom-call | tf_op jit(solution)/shard_map/pallas_call | solution.py:550

commit v2 on v1

--- a/solution.py
+++ b/solution.py
@@ -42,10 +42,10 @@
 
 
 def body(
-    tokens, cache, query_down, latent_down, query_up, key_up,
+    tokens, cache, query_down, latent_down, query_up, key_up, value_up,
     offset, bounds, freqs, query_gain, latent_gain,
     out,
-    xv, ldv, qdv, qupv, kupv, cos, sin,
+    xv, ldv, qdv, qupv, kupv, vupv, cos, sin,
     stage_kv, stage_q, rs_kv, rs_q, qc, ks, kc, kb, qn, qs, m_ref, l_ref, acc,
     load_sem, rs_send, rs_recv, qag_send, qag_recv, kag_send, kag_recv,
     cz_send, cz_recv, cp_send, cp_recv, bz_send, bz_recv, bp_send, bp_recv,
@@ -72,6 +72,7 @@
                 (cache, kc.at[pl.ds(0, CROWS)]),
                 (query_up, qupv),
                 (key_up, kupv),
+                (value_up, vupv),
             ]
         )
     ]
@@ -209,9 +210,15 @@
         start(cache_z(0, 0))
         start(cache_p(0, 0))
 
-        @pl.when(z > 0)
+        @pl.when(z == 0)
         def _():
-            cache_z(0, 1).start()
+            pl.semaphore_wait(ready_z.at[1], 1)
+
+        start(cache_z(0, 1))
+
+    for s in range(1, 3):
+        with scope(f"c{s}"):
+            cache_step(s)
 
     @pl.when(is_kv)
     def _():
@@ -234,6 +241,10 @@
                 mine, ks.at[0, rows], kag_send.at[d], kag_recv.at[group], head=(h + d) % NHEAD
             ).start()
 
+    for s in range(3, 5):
+        with scope(f"c{s}"):
+            cache_step(s)
+
     @pl.when(jnp.logical_not(is_kv))
     def _():
         total = stage_q[q_block]
@@ -249,16 +260,8 @@
                 head=(h + d) % NHEAD,
             ).start()
 
-    with scope("c12"):
-
-        @pl.when(z == 0)
-        def _():
-            pl.semaphore_wait(ready_z.at[1], 1)
-            cache_z(0, 1).start()
-
-        tail.append(cache_z(0, 1))
-        cache_step(1)
-        cache_step(2)
+    with scope("c5"):
+        cache_step(5)
 
     with scope("role"):
 
@@ -315,10 +318,12 @@
 
     block_step(0)
     kb[0, :ROWS] = ks[role]
-    for s in range(1, 6):
+    for s in range(1, 4):
         with scope(f"bc{s}"):
             block_step(s)
-            cache_step(s + 2)
+            cache_step(s + 5)
+    with scope("b4"):
+        block_step(4)
 
     for b in range(QBLOCKS):
         with scope("w_agq"):
@@ -412,51 +417,60 @@
                 for k in range(SUBS):
                     block_p(s, d, k).wait_recv()
 
-    with scope("h"):
-        for i in range(4):
-            two_heads(i)
+    def block_attends(low, high):
+        with scope(f"ba{low}"):
+
+            @pl.loop(low, high)
+            def _(s):
+                block_attend(s % 8)
+
+    def cache_attends(low, high):
+        with scope(f"ca{low}"):
+
+            @pl.loop(low, high)
+            def _(j):
+                cache_attend(j)
+
+    with scope("h01"):
+        two_heads(0)
+        two_heads(1)
+    with scope("b5"):
+        block_step(5)
+    with scope("h23"):
+        two_heads(2)
+        two_heads(3)
     with scope("b6"):
         block_step(6)
-        cache_step(8)
-    with scope("self"):
-        attend_self()
+    attend_self()
     with scope("cpw"):
         for s in range(9):
             cache_partner_wait(s)
-    with scope("ca01"):
-
-        @pl.loop(0, 2)
-        def _(j):
-            cache_attend(j)
-
+    cache_attends(0, 2)
     with scope("b7"):
         block_step(7)
-    with scope("ca23"):
-
-        @pl.loop(2, 4)
-        def _(j):
-            cache_attend(j)
-
+    cache_attends(2, 4)
+    with scope("bpw1"):
+        block_partner_wait(1)
+        block_partner_wait(2)
+    block_attends(1, 3)
     with scope("b8"):
         block_step(8)
-        for s in range(1, 7):
+        for s in range(3, 7):
             block_partner_wait(s)
-    with scope("ba16"):
-
-        @pl.loop(1, 7)
-        def _(s):
-            block_attend(s)
-
+    block_attends(3, 7)
     with scope("bpw"):
         for s in (7, 0, 8):
             block_partner_wait(s)
-    with scope("ba78"):
-
-        @pl.loop(7, 9)
-        def _(s):
-            block_attend(s % 8)
-
-    out[...] = (acc[...] / jnp.sum(l_ref[...], axis=0, keepdims=True)).astype(BF16)
+    block_attends(7, 9)
+
+    loads[6].wait()
+    scale = 1.0 / jnp.sum(l_ref[...], axis=0, keepdims=True)
+    for n in range(HEADS):
+        columns = slice(ROWS * n, ROWS * (n + 1))
+        olat = (acc[:, columns] * scale[:, columns]).astype(BF16)
+        out[:, VAL * n : VAL * (n + 1)] = lax.dot_general(
+            olat, vupv[n], (((0,), (0,)), ((), ())), preferred_element_type=F32
+        )
 
     for item in tail:
         if isinstance(item, tuple):
@@ -489,14 +503,6 @@
             ).wait_send()
 
 
-def values(olat, value_up, out):
-    for n in range(HEADS):
-        out[:, VAL * n : VAL * (n + 1)] = lax.dot_general(
-            olat[:, ROWS * n : ROWS * (n + 1)], value_up[n], (((0,), (0,)), ((), ())),
-            preferred_element_type=F32,
-        ).astype(BF16)
-
-
 def local(
     tokens, latent_cache, offset, bounds, query_down, latent_down_weight, query_gain,
     latent_norm_gain, query_up, key_up_transposed, value_up_weight,
@@ -509,10 +515,10 @@
     smem = pl.BlockSpec(memory_space=pltpu.SMEM)
     dma = lambda n: pltpu.SemaphoreType.DMA((n,))
     wide = HEADS * (NOPE + ROT)
-    olat = pl.pallas_call(
+    result = pl.pallas_call(
         body,
-        out_shape=jax.ShapeDtypeStruct((LAT, QCOLS), BF16),
-        in_specs=[anywhere] * 6 + [smem] + [vmem] * 4,
+        out_shape=jax.ShapeDtypeStruct((ROWS, HEADS * VAL), F32),
+        in_specs=[anywhere] * 7 + [smem] + [vmem] * 4,
         out_specs=vmem,
         scratch_shapes=[
             pltpu.VMEM((ROWS, tokens.shape[2]), BF16),
@@ -520,6 +526,7 @@
             pltpu.VMEM((tokens.shape[2], QRANK), BF16),
             pltpu.VMEM((QRANK, wide), BF16),
             pltpu.VMEM((HEADS, NOPE, LAT), BF16),
+            pltpu.VMEM((HEADS, LAT, VAL), BF16),
             pltpu.VMEM((ROWS, ROT), F32),
             pltpu.VMEM((ROWS, ROT), F32),
             pltpu.VMEM((ROWS, KEY), BF16),
@@ -535,7 +542,7 @@
             pltpu.VMEM((1, QCOLS), F32),
             pltpu.VMEM((8, QCOLS), F32),
             pltpu.VMEM((LAT, QCOLS), F32),
-            dma(6), dma(16), dma(16), dma(16), dma(12), dma(32), dma(8),
+            dma(7), dma(16), dma(16), dma(16), dma(12), dma(32), dma(8),
             dma(16), dma(16), dma(18), dma(18),
             dma(16 * SUBS), dma(16 * SUBS), dma(18 * SUBS), dma(18 * SUBS),
             pltpu.SemaphoreType.REGULAR((2,)), pltpu.SemaphoreType.REGULAR((1,)),
@@ -545,15 +552,9 @@
         ),
     )(
         tokens, latent_cache, query_down, latent_down_weight, query_up, key_up_transposed,
-        offset, bounds, freqs, query_gain, latent_norm_gain,
+        value_up_weight, offset, bounds, freqs, query_gain, latent_norm_gain,
     )
-    result = pl.pallas_call(
-        values,
-        out_shape=jax.ShapeDtypeStruct((ROWS, HEADS * VAL), BF16),
-        in_specs=[vmem, vmem],
-        out_specs=vmem,
-    )(olat, value_up_weight)
-    return result[None]
+    return result.astype(BF16)[None]
 
 
 def solution(mesh):

time: 89.4 us -> 88.5 us (0.990)
  the two profiles are of different devices: /device:TPU:6 before, /device:TPU:22 now
where the time goes in v2:
time: 88.5 us; the launch traced here: 88.3 us
  Pallas kernels  86 us (97%)
  other arithmetic  1.62 us (2%)
    pallas_call x1, Pallas kernels, local(): pl.pallas_call(body, out_shape=jax.ShapeDtypeStruct((ROWS, HEADS * VAL),...  86 us

profile of v2, /device:TPU:22, one launch (start us, length us, event | category | flops | bytes accessed | tf_op | source)
XLA Modules:
  0.0 88.3 jit_solution(5146325545625014941)
XLA Ops:
  0.7 86.0 %shard_map.118 = f32[64,1024]{1,0:T(8,128)} custom-call(bf16[1,64,448]{2,1,0:T(8,128)(2,1)} %tokens.1, bf16[48,576]{1,0:T(8,128)(2,1)} %cache.1, bf16[448,1536]{1,0:T(8,128)(2,1)} %query_down.1, bf16[448,576]{1,0:T(8,128)(2,1)} %latent_down.1, bf16[1536,1536]{1,0:T(8,128)(2,1)} %query_up.1, bf16[8,128,512]{2,1,0:T(8,128)(2,1)} %key_up.1, ...), custom_call_target="tpu_custom_call" | custom-call | tf_op jit(solution)/shard_map/pallas_call | solution.py:518
  86.7 1.6 %convert_bitcast_fusion = bf16[1,64,1024]{2,1,0:T(8,128)(2,1)} fusion(f32[64,1024]{1,0:T(8,128)} %shard_map.118), kind=kLoop, calls=%fused_computation | loop fusion | flops 65536 | bytes 393216 | tf_op jit(solution)/shard_map/broadcast_in_dim | solution.py:557

commit v3 on v2

--- a/solution.py
+++ b/solution.py
@@ -245,6 +245,64 @@
         with scope(f"c{s}"):
             cache_step(s)
 
+
+    with scope("role"):
+
+        @pl.when(gives == 1)
+        def _():
+            rows = pl.ds(pl.multiple_of(16 * group, 16), 16)
+            pl.semaphore_wait(ready_role.at[0], NHEAD)
+            for d in range(NHEAD):
+                remote(
+                    ks.at[0, rows], ks.at[1, rows], kag_send.at[NHEAD + d], kag_recv.at[4 + group],
+                    role=1, head=(h + d) % NHEAD,
+                ).start()
+
+    for g in range(4):
+        piece = ks.at[0, pl.ds(16 * g, 16)]
+
+        with scope("w_agkv"):
+
+            @pl.when(h != 4 * g + 3)
+            def _():
+                remote(piece, piece, kag_send.at[0], kag_recv.at[g], head=4 * g + 3).wait_recv()
+
+    @pl.when(role == 1)
+    def _():
+        for g in range(4):
+            piece = ks.at[1, pl.ds(16 * g, 16)]
+            with scope("w_agkv1"):
+                remote(piece, piece, kag_send.at[0], kag_recv.at[4 + g], role=0, head=4 * g + 3).wait_recv()
+
+    def block_rows(s, sub, k):
+        if s == 8:
+            s, sub = 0, sub + 1
+        return kb.at[s, pl.ds(sub * ROWS + k * PIECE, PIECE)]
+
+    def block_z(s, d, k):
+        i = (8 * d + s) * SUBS + k
+        src = ks.at[role, pl.ds(k * PIECE, PIECE)] if s == 0 else block_rows(s, d, k)
+        return remote(src, block_rows(s + 1, d, k), bz_send.at[i], bz_recv.at[i], ctx=(up, down)[d])
+
+    def block_p(s, d, k):
+        i = (9 * d + s) * SUBS + k
+        src = ks.at[role, pl.ds(k * PIECE, PIECE)] if s == 0 else block_rows(s, d, k)
+        return remote(src, block_rows(s, 2 + d, k), bp_send.at[i], bp_recv.at[i], ctx=partner)
+
+    def block_step(s):
+        for k in range(SUBS):
+            for d in range(2):
+                if 0 < s <= last[d]:
+                    block_z(s - 1, d, k).wait_recv()
+                if s < last[d]:
+                    start(block_z(s, d, k))
+                if s <= last[d] and (s > 0 or d == 0):
+                    start(block_p(s, d, k))
+
+    left = list(tail)
+    tail.clear()
+    block_step(0)
+
     @pl.when(jnp.logical_not(is_kv))
     def _():
         total = stage_q[q_block]
@@ -260,68 +318,39 @@
                 head=(h + d) % NHEAD,
             ).start()
 
+    kb[0, :ROWS] = ks[role]
     with scope("c5"):
         cache_step(5)
-
-    with scope("role"):
-
-        @pl.when(gives == 1)
-        def _():
-            rows = pl.ds(pl.multiple_of(16 * group, 16), 16)
-            pl.semaphore_wait(ready_role.at[0], NHEAD)
-            for d in range(NHEAD):
-                remote(
-                    ks.at[0, rows], ks.at[1, rows], kag_send.at[NHEAD + d], kag_recv.at[4 + group],
-                    role=1, head=(h + d) % NHEAD,
-                ).start()
-
-    for g in range(4):
-        piece = ks.at[0, pl.ds(16 * g, 16)]
-
-        with scope("w_agkv"):
-
-            @pl.when(h != 4 * g + 3)
-            def _():
-                remote(piece, piece, kag_send.at[0], kag_recv.at[g], head=4 * g + 3).wait_recv()
-
-    @pl.when(role == 1)
-    def _():
-        for g in range(4):
-            piece = ks.at[1, pl.ds(16 * g, 16)]
-            with scope("w_agkv1"):
-                remote(piece, piece, kag_send.at[0], kag_recv.at[4 + g], role=0, head=4 * g + 3).wait_recv()
-
-    def block_rows(s, sub, k):
-        if s == 8:
-            s, sub = 0, sub + 1
-        return kb.at[s, pl.ds(sub * ROWS + k * PIECE, PIECE)]
-
-    def block_z(s, d, k):
-        i = (8 * d + s) * SUBS + k
-        src = ks.at[role, pl.ds(k * PIECE, PIECE)] if s == 0 else block_rows(s, d, k)
-        return remote(src, block_rows(s + 1, d, k), bz_send.at[i], bz_recv.at[i], ctx=(up, down)[d])
-
-    def block_p(s, d, k):
-        i = (9 * d + s) * SUBS + k
-        src = ks.at[role, pl.ds(k * PIECE, PIECE)] if s == 0 else block_rows(s, d, k)
-        return remote(src, block_rows(s, 2 + d, k), bp_send.at[i], bp_recv.at[i], ctx=partner)
-
-    def block_step(s):
-        for k in range(SUBS):
-            for d in range(2):
-                if 0 < s <= last[d]:
-                    block_z(s - 1, d, k).wait_recv()
-                if s < last[d]:
-                    start(block_z(s, d, k))
-                if s <= last[d] and (s > 0 or d == 0):
-                    start(block_p(s, d, k))
-
-    block_step(0)
-    kb[0, :ROWS] = ks[role]
     for s in range(1, 4):
         with scope(f"bc{s}"):
             block_step(s)
             cache_step(s + 5)
+    def drain(items):
+        for item in items:
+            if isinstance(item, tuple):
+
+                @pl.when(item[0])
+                def _():
+                    item[1].wait_send()
+
+            else:
+                item.wait_send()
+
+    drain(left)
+
+    @pl.when(is_kv)
+    def _():
+        mine = ks.at[0, pl.ds(pl.multiple_of(16 * group, 16), 16)]
+        for d in range(1, NHEAD):
+            remote(mine, mine, kag_send.at[d], kag_recv.at[0], head=(h + d) % NHEAD).wait_send()
+
+        @pl.when(role == 0)
+        def _():
+            for d in range(NHEAD):
+                remote(
+                    mine, mine, kag_send.at[NHEAD + d], kag_recv.at[0], role=1, head=(h + d) % NHEAD
+                ).wait_send()
+
     with scope("b4"):
         block_step(4)
 
@@ -458,6 +487,14 @@
         for s in range(3, 7):
             block_partner_wait(s)
     block_attends(3, 7)
+
+    @pl.when(jnp.logical_not(is_kv))
+    def _():
+        for d in range(1, NHEAD):
+            remote(
+                qc.at[q_block], qc.at[q_block], qag_send.at[d], qag_recv.at[0], head=(h + d) % NHEAD
+            ).wait_send()
+
     with scope("bpw"):
         for s in (7, 0, 8):
             block_partner_wait(s)
@@ -472,35 +509,7 @@
             olat, vupv[n], (((0,), (0,)), ((), ())), preferred_element_type=F32
         )
 
-    for item in tail:
-        if isinstance(item, tuple):
-
-            @pl.when(item[0])
-            def _():
-                item[1].wait_send()
-
-        else:
-            item.wait_send()
-
-    @pl.when(is_kv)
-    def _():
-        mine = ks.at[0, pl.ds(pl.multiple_of(16 * group, 16), 16)]
-        for d in range(1, NHEAD):
-            remote(mine, mine, kag_send.at[d], kag_recv.at[0], head=(h + d) % NHEAD).wait_send()
-
-        @pl.when(role == 0)
-        def _():
-            for d in range(NHEAD):
-                remote(
-                    mine, mine, kag_send.at[NHEAD + d], kag_recv.at[0], role=1, head=(h + d) % NHEAD
-                ).wait_send()
-
-    @pl.when(jnp.logical_not(is_kv))
-    def _():
-        for d in range(1, NHEAD):
-            remote(
-                qc.at[q_block], qc.at[q_block], qag_send.at[d], qag_recv.at[0], head=(h + d) % NHEAD
-            ).wait_send()
+    drain(tail)
 
 
 def local(

time: 88.5 us -> 85.2 us (0.963)
  the two profiles are of different devices: /device:TPU:22 before, /device:TPU:6 now
where the time goes in v3:
time: 85.2 us; the launch traced here: 85 us
  Pallas kernels  82.7 us (97%)
  other arithmetic  1.62 us (2%)
    pallas_call x1, Pallas kernels, local(): pl.pallas_call(body, out_shape=jax.ShapeDtypeStruct((ROWS, HEADS * VAL),...  82.7 us

profile of v3, /device:TPU:6, one launch (start us, length us, event | category | flops | bytes accessed | tf_op | source)
XLA Modules:
  0.0 85.0 jit_solution(2423284001090701938)
XLA Ops:
  0.7 82.7 %shard_map.118 = f32[64,1024]{1,0:T(8,128)} custom-call(bf16[1,64,448]{2,1,0:T(8,128)(2,1)} %tokens.1, bf16[48,576]{1,0:T(8,128)(2,1)} %cache.1, bf16[448,1536]{1,0:T(8,128)(2,1)} %query_down.1, bf16[448,576]{1,0:T(8,128)(2,1)} %latent_down.1, bf16[1536,1536]{1,0:T(8,128)(2,1)} %query_up.1, bf16[8,128,512]{2,1,0:T(8,128)(2,1)} %key_up.1, ...), custom_call_target="tpu_custom_call" | custom-call | tf_op jit(solution)/shard_map/pallas_call | solution.py:527
  83.4 1.6 %convert_bitcast_fusion = bf16[1,64,1024]{2,1,0:T(8,128)(2,1)} fusion(f32[64,1024]{1,0:T(8,128)} %shard_map.118), kind=kLoop, calls=%fused_computation | loop fusion | flops 65536 | bytes 393216 | tf_op jit(solution)/shard_map/broadcast_in_dim | solution.py:566
